TPU v7x, 32 devices: a whole 2x2x4 slice. The times are simulated.
32 devices in a mesh: lat: 4 (over z), rad: 8 (over y, x, core).
Axes of the slice: x: 2, y: 2, z: 4, core: 2. Of those that a mesh axis runs over, the one named last changes fastest.
Arguments:
- positions: float32 [4096, 3, 128], P(('lat', 'rad')), may hold values from 0 to 1
- fields: bfloat16 [4096, 16, 128], P(('lat', 'rad')), may hold values from -6 to 6
- velocity: float32 [81, 8192], P(None, ('lat', 'rad')), may hold values from -3 to 3
- counts: int32 [32], P(('lat', 'rad')), may hold values from 1 to 128, as said below
- elements: int32 [3, 4096], P(None, ('lat', 'rad')), may hold values from 0 to 255
- routes: int32 [2, 4096], P(None, ('lat', 'rad')), may hold values from 0 to 239
Outputs:
- moved: float32 [7680, 3, 128], P(('lat', 'rad'))
- projected: float32 [27, 16, 8192], P(None, None, ('lat', 'rad'))
Inputs may be any that keep to these rules, and one draw needn't show every extreme that they name: counts[d] is at most 128 and equals 128 on some device.
All inputs are finite; a program needn't handle non-finite values.
Results may differ from a plain program's by a relative error of at most 0.0003.
Values sent between devices are 32-bit elements; how exact they have to be, the bound alone decides.
A program may use at most 64 MiB of HBM per device.

v0:
```python
import jax
import jax.numpy as jnp
from jax import lax
from jax.sharding import PartitionSpec as P

time_step = 0.4
exact = lax.Precision.HIGHEST


def passed_along(x, axis, by):
    size = lax.axis_size(axis)
    return lax.ppermute(x, axis, [(i, (i + by) % size) for i in range(size)])


def lagrange(coord):
    first_node = 2.0 * (coord - 0.5) * (coord - 1.0)
    middle_node = -4.0 * coord * (coord - 1.0)
    last_node = 2.0 * coord * (coord - 0.5)
    return jnp.stack([first_node, middle_node, last_node], axis=0)


def basis(points):
    along_x = lagrange(points[:, 0, :])
    along_y = lagrange(points[:, 1, :])
    along_z = lagrange(points[:, 2, :])
    table = along_x[:, None, None] * along_y[None, :, None] * along_z[None, None, :]
    return jnp.moveaxis(table.reshape(27, points.shape[0], points.shape[2]), 0, 1)


def speed(columns, points):
    coefficients = columns.T.reshape(points.shape[0], 3, 27)
    return jnp.einsum("scn,snb->scb", coefficients, basis(points), precision=exact)


def place_rows(target, valid, number):
    matches = (target[:, None] == jnp.arange(number, dtype=jnp.int32)[None, :]) & valid[:, None]
    present = jnp.any(matches, axis=0)
    source = jnp.sum(
        jnp.where(matches, jnp.arange(target.shape[0], dtype=jnp.int32)[:, None], 0), axis=0
    )
    return (source, present)


def arrange(cargo, source, present):
    result = []
    for member in cargo:
        picked = jnp.take(member, source, axis=0)
        layout = (present.shape[0],) + (1,) * (member.ndim - 1)
        result.append(jnp.where(present.reshape(layout), picked, jnp.zeros_like(picked)))
    return tuple(result)


def migrate(cargo, rad_count, capacity):
    kinds = tuple((member.dtype for member in cargo))
    shaped = tuple(
        (
            member.astype(jnp.float32).reshape((3, rad_count, capacity) + member.shape[1:])
            for member in cargo
        )
    )
    crossed = lax.all_to_all(shaped, "rad", split_axis=1, concat_axis=1, tiled=True)
    sheets = []
    for sheet_number in range(3):
        portion = tuple((member[sheet_number] for member in crossed))
        if sheet_number != 1:
            portion = passed_along(portion, "lat", sheet_number - 1)
        sheets.append(portion)
    moved = tuple(
        (
            jnp.stack([sheets[sheet_number][member_index] for sheet_number in range(3)])
            for member_index in range(len(cargo))
        )
    )
    result = []
    for member, kind in zip(moved, kinds):
        flat = member.reshape((3 * rad_count * capacity,) + member.shape[3:])
        result.append(flat.astype(jnp.int32) if kind == jnp.int32 else flat)
    return tuple(result)


def block_sums(points, carried):
    shapes = basis(points)
    moments = jnp.einsum("snb,sfb->snf", shapes, carried, precision=exact)
    return (moments, jnp.sum(shapes * shapes, axis=2))


def per_device(positions, fields, velocity, counts, elements, routes):
    rad_count = lax.axis_size("rad")
    blocks = positions.shape[0]
    capacity = max(1, 2 * blocks // (3 * rad_count))
    places = 3 * rad_count * capacity
    owned = velocity.shape[1]
    home_valid = jnp.arange(blocks, dtype=jnp.int32) < counts[0]
    first_speed = speed(jnp.take(velocity, elements[0], axis=1), positions)
    midway = positions + 0.5 * time_step * first_speed
    source, present = place_rows(routes[0], home_valid, places)
    wide_fields = fields.astype(jnp.float32)
    labels = jnp.stack([home_valid.astype(jnp.int32), elements[1], routes[1], elements[2]], axis=1)
    pairs = jnp.stack([positions, midway], axis=1)
    labels, pairs, carried = migrate(
        arrange((labels, pairs, wide_fields), source, present), rad_count, capacity
    )
    mid_valid = labels[:, 0] > 0
    second_speed = speed(jnp.take(velocity, labels[:, 1], axis=1), pairs[:, 1])
    landed = pairs[:, 0] + time_step * second_speed
    source, present = place_rows(labels[:, 2], mid_valid, places)
    tags = jnp.stack([mid_valid.astype(jnp.int32), labels[:, 3]], axis=1)
    moments, weights_sum = block_sums(landed, carried)
    tags, arrived, moments, weights_sum = migrate(
        arrange((tags, landed, moments, weights_sum), source, present), rad_count, capacity
    )
    final_valid = tags[:, 0] > 0
    hits = (
        (tags[:, 1][:, None] == jnp.arange(owned, dtype=jnp.int32)[None, :]) & final_valid[:, None]
    ).astype(jnp.float32)
    totals = jnp.einsum("se,snf->nfe", hits, moments, precision=exact)
    weights = jnp.einsum("se,sn->ne", hits, weights_sum, precision=exact)
    projected = totals / (1.0 + weights[:, None, :])
    return (arrived, projected)


def solution(mesh):
    in_specs = (
        P(("lat", "rad"), None, None),
        P(("lat", "rad"), None, None),
        P(None, ("lat", "rad")),
        P(("lat", "rad")),
        P(None, ("lat", "rad")),
        P(None, ("lat", "rad")),
    )
    out_specs = (P(("lat", "rad"), None, None), P(None, None, ("lat", "rad")))
    return jax.shard_map(
        per_device, mesh=mesh, in_specs=in_specs, out_specs=out_specs, check_vma=False
    )
```

profile of v0, /device:TPU:0, one launch (start us, length us, event | category | flops | bytes accessed | tf_op | source)
XLA Modules:
  0.0 182.4 jit_solution(13250675665100041835)
XLA Ops:
  4.3 5.2 %all-to-all-start = ((f32[3,8,10,4]{2,3,0,1:T(4,128)}), f32[3,8,10,4]{2,3,0,1:T(4,128)S(1)}, u32[]{:S(2)}, u32[]{:S(2)}) async-start(f32[3,8,10,4]{2,3,0,1:T(4,128)} %copy.368), calls=%async_computation | async-start | bytes 98304 | tf_op jit(solution)/shard_map/all_to_all | solution.py:61
  13.1 2.7 %fusion.13 = f32[128,1,3,128]{3,2,0,1:T(4,128)S(1)} fusion(f32[128,3,27]{2,1,0:T(4,128)S(1)} %reshape.932, f32[128,27,128]{2,0,1:T(8,128)S(1)} %bitcast.202, f32[128,3,128]{2,0,1:T(8,128)S(1)} %copy-done), kind=kOutput, calls=%fused_computation.26 | convolution fusion | flops 16023552 | bytes 2204160 | tf_op jit(solution)/shard_map/scn,snb->scb/dot_general | solution.py:32
  17.7 2.2 %collective-permute-start = (f32[8,10,4]{1,0,2:T(8,128)S(1)}, f32[8,10,4]{1,0,2:T(8,128)S(1)}, u32[]{:S(2)}, u32[]{:S(2)}) collective-permute-start(f32[8,10,4]{1,0,2:T(8,128)S(1)} %bitcast.225), channel_id=1, source_target_pairs={{0,24},{8,0},{16,8},{24,16},{1,25},{9,1},{17,9},{25,17},{2,26},{10... | collective-permute-start | bytes 3848 | tf_op jit(solution)/shard_map/ppermute | solution.py:12
  24.1 4.2 %all-to-all-start.5 = ((f32[3,8,10,2]{2,3,0,1:T(2,128)}), f32[3,8,10,2]{2,3,0,1:T(2,128)S(1)}, u32[]{:S(2)}, u32[]{:S(2)}) async-start(f32[3,8,10,2]{2,3,0,1:T(2,128)} %copy.408), calls=%async_computation.5 | async-start | bytes 49152 | tf_op jit(solution)/shard_map/all_to_all | solution.py:61
  28.2 1.9 %fusion.16 = f32[3,8,10,2,3,128]{5,3,4,2,0,1:T(2,128)} fusion(f32[3,8,10,2,3,128]{5,4,3,2,1,0:T(4,128)S(1)} %bitcast.207, pred[3,8,10]{2,0,1:T(4,128)(4,1)S(1)} %copy.374, pred[3,8,10]{2,0,1:T(4,128)(4,1)S(1)} %copy.373), kind=kLoop, calls=%fused_computation.31 | loop fusion | flops 368640 | bytes 1475040 | tf_op jit(solution)/shard_map/jit(_where)/select_n | solution.py:49
  33.0 3.5 %all-to-all-start.1 = ((f32[3,8,10,2,3,128]{5,3,4,2,0,1:T(2,128)}), f32[3,8,10,2,3,128]{5,3,4,2,0,1:T(2,128)S(1)}, u32[]{:S(2)}, u32[]{:S(2)}) async-start(f32[3,8,10,2,3,128]{5,3,4,2,0,1:T(2,128)} %fusion.16), calls=%async_computation.1 | async-start | bytes 1474560 | tf_op jit(solution)/shard_map/all_to_all | solution.py:61
  40.9 2.5 %collective-permute-start.10 = (f32[8,10,2]{1,0,2:T(8,128)S(1)}, f32[8,10,2]{1,0,2:T(8,128)S(1)}, u32[]{:S(2)}, u32[]{:S(2)}) collective-permute-start(f32[8,10,2]{1,0,2:T(8,128)S(1)} %bitcast.233), channel_id=1, source_target_pairs={{0,24},{8,0},{16,8},{24,16},{1,25},{9,1},{17,9},{25,17},{2,26},{10... | collective-permute-start | bytes 1928 | tf_op jit(solution)/shard_map/ppermute | solution.py:12
  43.4 5.1 %all-to-all-done.1 = f32[3,8,10,2,3,128]{5,3,4,2,0,1:T(2,128)S(1)} async-done(((f32[3,8,10,2,3,128]{5,3,4,2,0,1:T(2,128)}), f32[3,8,10,2,3,128]{5,3,4,2,0,1:T(2,128)S(1)}, u32[]{:S(2)}, u32[]{:S(2)}) %all-to-all-start.1) | async-done | bytes 737312 | tf_op jit(solution)/shard_map/all_to_all | solution.py:61
  48.5 4.3 %all-to-all-start.3 = ((f32[3,8,10,16,128]{4,3,2,0,1:T(8,128)}), f32[3,8,10,16,128]{4,3,2,0,1:T(8,128)}, u32[]{:S(2)}, u32[]{:S(2)}) async-start(f32[3,8,10,16,128]{4,3,2,0,1:T(8,128)} %copy.399), calls=%async_computation.3 | async-start | bytes 3932160 | tf_op jit(solution)/shard_map/all_to_all | solution.py:61
  53.1 3.9 %collective-permute-start.2 = (f32[8,10,2,3,128]{4,2,3,1,0:T(2,128)S(1)}, f32[8,10,2,3,128]{4,2,3,1,0:T(2,128)S(1)}, u32[]{:S(2)}, u32[]{:S(2)}) collective-permute-start(f32[8,10,2,3,128]{4,2,3,1,0:T(2,128)S(1)} %get-tuple-element.12), channel_id=1, source_target_pairs={{0,24},{8,0},{16,8},{24,16},{1,25},{9,1},{17,9},{25,17},{2,26},{10... | collective-permute-start | bytes 737288 | tf_op jit(solution)/shard_map/ppermute | solution.py:12
  57.5 5.9 %collective-permute-done.2 = f32[8,10,2,3,128]{4,2,3,1,0:T(2,128)S(1)} collective-permute-done((f32[8,10,2,3,128]{4,2,3,1,0:T(2,128)S(1)}, f32[8,10,2,3,128]{4,2,3,1,0:T(2,128)S(1)}, u32[]{:S(2)}, u32[]{:S(2)}) %collective-permute-start.2) | collective-permute-done | bytes 245792 | tf_op jit(solution)/shard_map/ppermute | solution.py:12
  63.4 5.4 %collective-permute-done.3 = f32[8,10,2,3,128]{4,2,3,1,0:T(2,128)S(1)} collective-permute-done((f32[8,10,2,3,128]{4,2,3,1,0:T(2,128)S(1)}, f32[8,10,2,3,128]{4,2,3,1,0:T(2,128)S(1)}, u32[]{:S(2)}, u32[]{:S(2)}) %collective-permute-start.3) | collective-permute-done | bytes 245792 | tf_op jit(solution)/shard_map/ppermute | solution.py:12
  70.2 4.1 %fusion.2 = f32[240,3,128]{2,1,0:T(4,128)S(1)} fusion(f32[240,3,27]{2,1,0:T(4,128)S(1)} %reshape.933, f32[240,27,128]{2,0,1:T(8,128)S(1)} %bitcast.201), kind=kOutput, calls=%fused_computation.11 | convolution fusion | flops 29859840 | bytes 3764160 | tf_op jit(solution)/shard_map/scn,snb->scb/dot_general | solution.py:32
  80.2 2.8 %slice_bitcast_fusion.5 = (f32[8,10,16,128]{3,2,1,0:T(8,128)}, f32[8,10,16,128]{3,2,1,0:T(8,128)}, f32[1,8,10,16,128]{4,3,2,1,0:T(8,128)}) fusion(f32[3,8,10,16,128]{4,3,2,0,1:T(8,128)} %all-to-all-done.3), kind=kLoop, calls=%fused_computation.37 | loop fusion | bytes 3932160 | tf_op jit(solution)/shard_map/squeeze | solution.py:64
  83.0 2.0 %collective-permute-start.6 = (f32[8,10,16,128]{3,2,1,0:T(8,128)}, f32[8,10,16,128]{3,2,1,0:T(8,128)}, u32[]{:S(2)}, u32[]{:S(2)}) collective-permute-start(f32[8,10,16,128]{3,2,1,0:T(8,128)} %get-tuple-element.7), channel_id=1, source_target_pairs={{0,24},{8,0},{16,8},{24,16},{1,25},{9,1},{17,9},{25,17},{2,26},{10... | collective-permute-start | bytes 1966088 | tf_op jit(solution)/shard_map/ppermute | solution.py:12
  86.1 3.8 %all-to-all-start.6 = ((f32[8,1,810]{2,1,0:T(1,128)}), f32[8,1,810]{2,1,0:T(1,128)S(1)}, u32[]{:S(2)}, u32[]{:S(2)}) async-start(f32[8,1,810]{2,1,0:T(1,128)} %reshape.939), calls=%async_computation.6 | async-start | bytes 57344 | tf_op jit(solution)/shard_map/all_to_all | solution.py:61
  92.2 2.6 %all-to-all-done.6 = f32[8,1,810]{2,1,0:T(1,128)S(1)} async-done(((f32[8,1,810]{2,1,0:T(1,128)}), f32[8,1,810]{2,1,0:T(1,128)S(1)}, u32[]{:S(2)}, u32[]{:S(2)}) %all-to-all-start.6) | async-done | bytes 25952 | tf_op jit(solution)/shard_map/all_to_all | solution.py:61
  94.7 4.2 %all-to-all-start.2 = ((f32[3,8,10,3,128]{4,3,2,0,1:T(4,128)}), f32[3,8,10,3,128]{4,3,2,0,1:T(4,128)}, u32[]{:S(2)}, u32[]{:S(2)}) async-start(f32[3,8,10,3,128]{4,3,2,0,1:T(4,128)} %copy.393), calls=%async_computation.2 | async-start | bytes 983040 | tf_op jit(solution)/shard_map/all_to_all | solution.py:61
  100.4 1.8 %collective-permute-start.13 = (f32[8,10,27]{2,0,1:T(8,128)S(1)}, f32[8,10,27]{2,0,1:T(8,128)S(1)}, u32[]{:S(2)}, u32[]{:S(2)}) collective-permute-start(f32[8,10,27]{2,0,1:T(8,128)S(1)} %bitcast.222), channel_id=1, source_target_pairs={{0,8},{8,16},{16,24},{24,0},{1,9},{9,17},{17,25},{25,1},{2,10},{10... | collective-permute-start | bytes 25928 | tf_op jit(solution)/shard_map/ppermute | solution.py:12
  102.2 2.3 %collective-permute-start.12 = (f32[8,10,27]{2,0,1:T(8,128)S(1)}, f32[8,10,27]{2,0,1:T(8,128)S(1)}, u32[]{:S(2)}, u32[]{:S(2)}) collective-permute-start(f32[8,10,27]{2,0,1:T(8,128)S(1)} %bitcast.221), channel_id=1, source_target_pairs={{0,24},{8,0},{16,8},{24,16},{1,25},{9,1},{17,9},{25,17},{2,26},{10... | collective-permute-start | bytes 25928 | tf_op jit(solution)/shard_map/ppermute | solution.py:12
  104.5 10.3 %collective-permute-done.7 = f32[8,10,16,128]{3,2,1,0:T(8,128)} collective-permute-done((f32[8,10,16,128]{3,2,1,0:T(8,128)}, f32[8,10,16,128]{3,2,1,0:T(8,128)}, u32[]{:S(2)}, u32[]{:S(2)}) %collective-permute-start.7) | collective-permute-done | bytes 655392 | tf_op jit(solution)/shard_map/ppermute | solution.py:12
  116.5 8.2 %fusion = f32[240,27,16]{1,2,0:T(8,128)} fusion(f32[240,16,128]{2,1,0:T(8,128)S(1)} %bitcast.206, f32[240,27,128]{2,0,1:T(8,128)S(1)} %bitcast.199), kind=kOutput, calls=%fused_computation.9 | convolution fusion | flops 159252480 | bytes 5698560 | tf_op jit(solution)/shard_map/snb,sfb->snf/dot_general | solution.py:83
  124.6 2.3 %gather_fusion.6 = f32[240,27,16]{1,2,0:T(8,128)S(1)} fusion(f32[240,27,16]{1,2,0:T(8,128)} %fusion, s32[1024]{0:T(1024)S(1)} %pad_clamp_fusion), kind=kCustom, calls=%fused_computation.6 | custom fusion | bytes 830400 | tf_op jit(solution)/shard_map/jit(_take)/gather | solution.py:47
  126.9 2.2 %fusion.37 = f32[8,3,10,16,27]{4,3,2,1,0:T(8,128)} fusion(f32[3,8,10,27,16]{3,4,2,1,0:T(8,128)S(1)} %bitcast.200, pred[3,8,10]{2,0,1:T(4,128)(4,1)S(1)} %copy.398, pred[3,8,10]{2,0,1:T(4,128)(4,1)S(1)} %copy.397), kind=kLoop, calls=%fused_computation.153 | loop fusion | flops 207360 | bytes 829920
  129.1 4.0 %reshape.937 = f32[8,1,12960]{2,1,0:T(1,128)} reshape(f32[8,3,10,16,27]{4,3,2,1,0:T(8,128)} %fusion.37) | data formatting | bytes 829440
  133.1 3.6 %all-to-all-start.4 = ((f32[8,1,12960]{2,1,0:T(1,128)}), f32[8,1,12960]{2,1,0:T(1,128)S(1)}, u32[]{:S(2)}, u32[]{:S(2)}) async-start(f32[8,1,12960]{2,1,0:T(1,128)} %reshape.937), calls=%async_computation.4 | async-start | bytes 835584 | tf_op jit(solution)/shard_map/all_to_all | solution.py:61
  138.0 2.0 %collective-permute-start.4 = (f32[8,10,3,128]{3,2,1,0:T(4,128)S(1)}, f32[8,10,3,128]{3,2,1,0:T(4,128)S(1)}, u32[]{:S(2)}, u32[]{:S(2)}) collective-permute-start(f32[8,10,3,128]{3,2,1,0:T(4,128)S(1)} %get-tuple-element.15), channel_id=1, source_target_pairs={{0,24},{8,0},{16,8},{24,16},{1,25},{9,1},{17,9},{25,17},{2,26},{10... | collective-permute-start | bytes 368648 | tf_op jit(solution)/shard_map/ppermute | solution.py:12
  140.1 5.2 %all-to-all-done.4 = f32[8,1,12960]{2,1,0:T(1,128)S(1)} async-done(((f32[8,1,12960]{2,1,0:T(1,128)}), f32[8,1,12960]{2,1,0:T(1,128)S(1)}, u32[]{:S(2)}, u32[]{:S(2)}) %all-to-all-start.4) | async-done | bytes 414752 | tf_op jit(solution)/shard_map/all_to_all | solution.py:61
  146.9 2.0 %reshape.938 = f32[8,3,10,16,27]{4,3,2,1,0:T(8,128)S(1)} reshape(f32[8,12960]{1,0:T(8,128)S(1)} %reduce.6) | data formatting | bytes 829440
  149.1 2.0 %collective-permute-start.8 = (f32[8,10,27,16]{2,3,1,0:T(8,128)S(1)}, f32[8,10,27,16]{2,3,1,0:T(8,128)S(1)}, u32[]{:S(2)}, u32[]{:S(2)}) collective-permute-start(f32[8,10,27,16]{2,3,1,0:T(8,128)S(1)} %get-tuple-element.4), channel_id=1, source_target_pairs={{0,24},{8,0},{16,8},{24,16},{1,25},{9,1},{17,9},{25,17},{2,26},{10... | collective-permute-start | bytes 414728 | tf_op jit(solution)/shard_map/ppermute | solution.py:12
  152.4 13.8 %collective-permute-done.8 = f32[8,10,27,16]{2,3,1,0:T(8,128)S(1)} collective-permute-done((f32[8,10,27,16]{2,3,1,0:T(8,128)S(1)}, f32[8,10,27,16]{2,3,1,0:T(8,128)S(1)}, u32[]{:S(2)}, u32[]{:S(2)}) %collective-permute-start.8) | collective-permute-done | bytes 138272 | tf_op jit(solution)/shard_map/ppermute | solution.py:12
  166.2 13.7 %collective-permute-done.9 = f32[8,10,27,16]{2,3,1,0:T(8,128)S(1)} collective-permute-done((f32[8,10,27,16]{2,3,1,0:T(8,128)S(1)}, f32[8,10,27,16]{2,3,1,0:T(8,128)S(1)}, u32[]{:S(2)}, u32[]{:S(2)}) %collective-permute-start.9) | collective-permute-done | bytes 138272 | tf_op jit(solution)/shard_map/ppermute | solution.py:12
  (145 shorter events, 40.7 us)
Async XLA Ops:
  0.6 12.1 %copy-start = (f32[128,3,128]{2,0,1:T(8,128)S(1)}, f32[128,3,128]{2,0,1:T(8,128)}, u32[]{:S(2)}) copy-start(f32[128,3,128]{2,0,1:T(8,128)} %param.6) | copy-start | bytes 589828
  4.3 11.7 %all-to-all-start = ((f32[3,8,10,4]{2,3,0,1:T(4,128)}), f32[3,8,10,4]{2,3,0,1:T(4,128)S(1)}, u32[]{:S(2)}, u32[]{:S(2)}) async-start(f32[3,8,10,4]{2,3,0,1:T(4,128)} %copy.368), calls=%async_computation | async-start | bytes 98304 | tf_op jit(solution)/shard_map/all_to_all | solution.py:61
  16.0 5.6 %collective-permute-start.1 = (f32[8,10,4]{1,0,2:T(8,128)S(1)}, f32[8,10,4]{1,0,2:T(8,128)S(1)}, u32[]{:S(2)}, u32[]{:S(2)}) collective-permute-start(f32[8,10,4]{1,0,2:T(8,128)S(1)} %bitcast.226), channel_id=1, source_target_pairs={{0,8},{8,16},{16,24},{24,0},{1,9},{9,17},{17,25},{25,1},{2,10},{10... | collective-permute-start | bytes 3848 | tf_op jit(solution)/shard_map/ppermute | solution.py:12
  17.7 4.0 %collective-permute-start = (f32[8,10,4]{1,0,2:T(8,128)S(1)}, f32[8,10,4]{1,0,2:T(8,128)S(1)}, u32[]{:S(2)}, u32[]{:S(2)}) collective-permute-start(f32[8,10,4]{1,0,2:T(8,128)S(1)} %bitcast.225), channel_id=1, source_target_pairs={{0,24},{8,0},{16,8},{24,16},{1,25},{9,1},{17,9},{25,17},{2,26},{10... | collective-permute-start | bytes 3848 | tf_op jit(solution)/shard_map/ppermute | solution.py:12
  24.1 9.0 %all-to-all-start.5 = ((f32[3,8,10,2]{2,3,0,1:T(2,128)}), f32[3,8,10,2]{2,3,0,1:T(2,128)S(1)}, u32[]{:S(2)}, u32[]{:S(2)}) async-start(f32[3,8,10,2]{2,3,0,1:T(2,128)} %copy.408), calls=%async_computation.5 | async-start | bytes 49152 | tf_op jit(solution)/shard_map/all_to_all | solution.py:61
  33.0 15.5 %all-to-all-start.1 = ((f32[3,8,10,2,3,128]{5,3,4,2,0,1:T(2,128)}), f32[3,8,10,2,3,128]{5,3,4,2,0,1:T(2,128)S(1)}, u32[]{:S(2)}, u32[]{:S(2)}) async-start(f32[3,8,10,2,3,128]{5,3,4,2,0,1:T(2,128)} %fusion.16), calls=%async_computation.1 | async-start | bytes 1474560 | tf_op jit(solution)/shard_map/all_to_all | solution.py:61
  39.5 17.9 %collective-permute-start.11 = (f32[8,10,2]{1,0,2:T(8,128)S(1)}, f32[8,10,2]{1,0,2:T(8,128)S(1)}, u32[]{:S(2)}, u32[]{:S(2)}) collective-permute-start(f32[8,10,2]{1,0,2:T(8,128)S(1)} %bitcast.234), channel_id=1, source_target_pairs={{0,8},{8,16},{16,24},{24,0},{1,9},{9,17},{17,25},{25,1},{2,10},{10... | collective-permute-start | bytes 1928 | tf_op jit(solution)/shard_map/ppermute | solution.py:12
  40.9 16.5 %collective-permute-start.10 = (f32[8,10,2]{1,0,2:T(8,128)S(1)}, f32[8,10,2]{1,0,2:T(8,128)S(1)}, u32[]{:S(2)}, u32[]{:S(2)}) collective-permute-start(f32[8,10,2]{1,0,2:T(8,128)S(1)} %bitcast.233), channel_id=1, source_target_pairs={{0,24},{8,0},{16,8},{24,16},{1,25},{9,1},{17,9},{25,17},{2,26},{10... | collective-permute-start | bytes 1928 | tf_op jit(solution)/shard_map/ppermute | solution.py:12
  48.5 31.6 %all-to-all-start.3 = ((f32[3,8,10,16,128]{4,3,2,0,1:T(8,128)}), f32[3,8,10,16,128]{4,3,2,0,1:T(8,128)}, u32[]{:S(2)}, u32[]{:S(2)}) async-start(f32[3,8,10,16,128]{4,3,2,0,1:T(8,128)} %copy.399), calls=%async_computation.3 | async-start | bytes 3932160 | tf_op jit(solution)/shard_map/all_to_all | solution.py:61
  53.1 10.3 %collective-permute-start.2 = (f32[8,10,2,3,128]{4,2,3,1,0:T(2,128)S(1)}, f32[8,10,2,3,128]{4,2,3,1,0:T(2,128)S(1)}, u32[]{:S(2)}, u32[]{:S(2)}) collective-permute-start(f32[8,10,2,3,128]{4,2,3,1,0:T(2,128)S(1)} %get-tuple-element.12), channel_id=1, source_target_pairs={{0,24},{8,0},{16,8},{24,16},{1,25},{9,1},{17,9},{25,17},{2,26},{10... | collective-permute-start | bytes 737288 | tf_op jit(solution)/shard_map/ppermute | solution.py:12
  57.0 11.8 %collective-permute-start.3 = (f32[8,10,2,3,128]{4,2,3,1,0:T(2,128)S(1)}, f32[8,10,2,3,128]{4,2,3,1,0:T(2,128)S(1)}, u32[]{:S(2)}, u32[]{:S(2)}) collective-permute-start(f32[8,10,2,3,128]{4,2,3,1,0:T(2,128)S(1)} %get-tuple-element.13), channel_id=1, source_target_pairs={{0,8},{8,16},{16,24},{24,0},{1,9},{9,17},{17,25},{25,1},{2,10},{10... | collective-permute-start | bytes 737288 | tf_op jit(solution)/shard_map/ppermute | solution.py:12
  83.0 21.5 %collective-permute-start.6 = (f32[8,10,16,128]{3,2,1,0:T(8,128)}, f32[8,10,16,128]{3,2,1,0:T(8,128)}, u32[]{:S(2)}, u32[]{:S(2)}) collective-permute-start(f32[8,10,16,128]{3,2,1,0:T(8,128)} %get-tuple-element.7), channel_id=1, source_target_pairs={{0,24},{8,0},{16,8},{24,16},{1,25},{9,1},{17,9},{25,17},{2,26},{10... | collective-permute-start | bytes 1966088 | tf_op jit(solution)/shard_map/ppermute | solution.py:12
  85.0 29.8 %collective-permute-start.7 = (f32[8,10,16,128]{3,2,1,0:T(8,128)}, f32[8,10,16,128]{3,2,1,0:T(8,128)}, u32[]{:S(2)}, u32[]{:S(2)}) collective-permute-start(f32[8,10,16,128]{3,2,1,0:T(8,128)} %get-tuple-element.8), channel_id=1, source_target_pairs={{0,8},{8,16},{16,24},{24,0},{1,9},{9,17},{17,25},{25,1},{2,10},{10... | collective-permute-start | bytes 1966088 | tf_op jit(solution)/shard_map/ppermute | solution.py:12
  86.1 8.7 %all-to-all-start.6 = ((f32[8,1,810]{2,1,0:T(1,128)}), f32[8,1,810]{2,1,0:T(1,128)S(1)}, u32[]{:S(2)}, u32[]{:S(2)}) async-start(f32[8,1,810]{2,1,0:T(1,128)} %reshape.939), calls=%async_computation.6 | async-start | bytes 57344 | tf_op jit(solution)/shard_map/all_to_all | solution.py:61
  94.7 38.4 %all-to-all-start.2 = ((f32[3,8,10,3,128]{4,3,2,0,1:T(4,128)}), f32[3,8,10,3,128]{4,3,2,0,1:T(4,128)}, u32[]{:S(2)}, u32[]{:S(2)}) async-start(f32[3,8,10,3,128]{4,3,2,0,1:T(4,128)} %copy.393), calls=%async_computation.2 | async-start | bytes 983040 | tf_op jit(solution)/shard_map/all_to_all | solution.py:61
  100.4 36.4 %collective-permute-start.13 = (f32[8,10,27]{2,0,1:T(8,128)S(1)}, f32[8,10,27]{2,0,1:T(8,128)S(1)}, u32[]{:S(2)}, u32[]{:S(2)}) collective-permute-start(f32[8,10,27]{2,0,1:T(8,128)S(1)} %bitcast.222), channel_id=1, source_target_pairs={{0,8},{8,16},{16,24},{24,0},{1,9},{9,17},{17,25},{25,1},{2,10},{10... | collective-permute-start | bytes 25928 | tf_op jit(solution)/shard_map/ppermute | solution.py:12
  102.2 34.5 %collective-permute-start.12 = (f32[8,10,27]{2,0,1:T(8,128)S(1)}, f32[8,10,27]{2,0,1:T(8,128)S(1)}, u32[]{:S(2)}, u32[]{:S(2)}) collective-permute-start(f32[8,10,27]{2,0,1:T(8,128)S(1)} %bitcast.221), channel_id=1, source_target_pairs={{0,24},{8,0},{16,8},{24,16},{1,25},{9,1},{17,9},{25,17},{2,26},{10... | collective-permute-start | bytes 25928 | tf_op jit(solution)/shard_map/ppermute | solution.py:12
  133.1 12.2 %all-to-all-start.4 = ((f32[8,1,12960]{2,1,0:T(1,128)}), f32[8,1,12960]{2,1,0:T(1,128)S(1)}, u32[]{:S(2)}, u32[]{:S(2)}) async-start(f32[8,1,12960]{2,1,0:T(1,128)} %reshape.937), calls=%async_computation.4 | async-start | bytes 835584 | tf_op jit(solution)/shard_map/all_to_all | solution.py:61
  138.0 13.5 %collective-permute-start.4 = (f32[8,10,3,128]{3,2,1,0:T(4,128)S(1)}, f32[8,10,3,128]{3,2,1,0:T(4,128)S(1)}, u32[]{:S(2)}, u32[]{:S(2)}) collective-permute-start(f32[8,10,3,128]{3,2,1,0:T(4,128)S(1)} %get-tuple-element.15), channel_id=1, source_target_pairs={{0,24},{8,0},{16,8},{24,16},{1,25},{9,1},{17,9},{25,17},{2,26},{10... | collective-permute-start | bytes 368648 | tf_op jit(solution)/shard_map/ppermute | solution.py:12
  140.0 11.5 %collective-permute-start.5 = (f32[8,10,3,128]{3,2,1,0:T(4,128)S(1)}, f32[8,10,3,128]{3,2,1,0:T(4,128)S(1)}, u32[]{:S(2)}, u32[]{:S(2)}) collective-permute-start(f32[8,10,3,128]{3,2,1,0:T(4,128)S(1)} %get-tuple-element.16), channel_id=1, source_target_pairs={{0,8},{8,16},{16,24},{24,0},{1,9},{9,17},{17,25},{25,1},{2,10},{10... | collective-permute-start | bytes 368648 | tf_op jit(solution)/shard_map/ppermute | solution.py:12
  149.1 17.1 %collective-permute-start.8 = (f32[8,10,27,16]{2,3,1,0:T(8,128)S(1)}, f32[8,10,27,16]{2,3,1,0:T(8,128)S(1)}, u32[]{:S(2)}, u32[]{:S(2)}) collective-permute-start(f32[8,10,27,16]{2,3,1,0:T(8,128)S(1)} %get-tuple-element.4), channel_id=1, source_target_pairs={{0,24},{8,0},{16,8},{24,16},{1,25},{9,1},{17,9},{25,17},{2,26},{10... | collective-permute-start | bytes 414728 | tf_op jit(solution)/shard_map/ppermute | solution.py:12
  151.1 28.8 %collective-permute-start.9 = (f32[8,10,27,16]{2,3,1,0:T(8,128)S(1)}, f32[8,10,27,16]{2,3,1,0:T(8,128)S(1)}, u32[]{:S(2)}, u32[]{:S(2)}) collective-permute-start(f32[8,10,27,16]{2,3,1,0:T(8,128)S(1)} %get-tuple-element.5), channel_id=1, source_target_pairs={{0,8},{8,16},{16,24},{24,0},{1,9},{9,17},{17,25},{25,1},{2,10},{10... | collective-permute-start | bytes 414728 | tf_op jit(solution)/shard_map/ppermute | solution.py:12
where the time goes:
time: 183 us; the launch traced here: 182 us
  waiting for transfers between devices  62.9 us (34%)
  starting transfers between devices  50.8 us (28%)
  local copies, waits for them, and re-layouts  33.4 us (18%)
  other arithmetic  16.6 us (9%)
  matrix products  16.5 us (9%)
  between operations  2.14 us (1%)
    ppermute x14, waiting for transfers between devices, passed_along(): return lax.ppermute(x, axis, [(i, (i + by) % size) for i in range(size)])  49.3 us
    all_to_all x7, starting transfers between devices, migrate(): lax.all_to_all(shaped, 'rad', split_axis=1, concat_axis=1, tiled=True)  28.8 us
    ppermute x14, starting transfers between devices, passed_along(): return lax.ppermute(x, axis, [(i, (i + by) % size) for i in range(size)])  22 us
    all_to_all x7, waiting for transfers between devices, migrate(): lax.all_to_all(shaped, 'rad', split_axis=1, concat_axis=1, tiled=True)  13.6 us
    gather x12, local copies, waits for them, and re-layouts, arrange(): picked = jnp.take(member, source, axis=0)  10.3 us
    dot_general x1, matrix products, block_sums(): moments = jnp.einsum('snb,sfb->snf', shapes, carried, precision=exact)  8.16 us
    unnamed x18, local copies, waits for them, and re-layouts  8.14 us
    dot_general x2, matrix products, speed(): jnp.einsum('scn,snb->scb', coefficients, basis(points), precision=exact)  6.78 us
  transfers between devices with their start and end apart: 21, of which 10 were waited for; matrix products, arithmetic and copies ran while one was open for 31% of the time, Pallas kernels for 0%

commit v1 on v0

v1 whole, which is shorter than its diff:
```python
import functools

import jax
import jax.numpy as jnp
from jax import lax
from jax.experimental import pallas as pl
from jax.experimental.pallas import tpu as pltpu
from jax.sharding import PartitionSpec as P

time_step = 0.4
MESH = pl.DeviceIdType.MESH
LANES = 128


def round_up(x, by):
    return -(-x // by) * by


def split(x):
    high = x.astype(jnp.bfloat16)
    low = (x - high.astype(jnp.float32)).astype(jnp.bfloat16)
    return high, low


def dot(a, b, dims):
    return lax.dot_general(a, b, (dims, ((), ())), preferred_element_type=jnp.float32)


def lagrange(s):
    return (2.0 * (s - 0.5) * (s - 1.0), -4.0 * s * (s - 1.0), 2.0 * s * (s - 0.5))


def advance(points_in, coefficients, base, out, scale, group):
    markers = base.shape[1]

    def step(g, carry):
        rows = pl.ds(pl.multiple_of(g * group, group), group)
        lx = lagrange(points_in[0, rows, :])
        ly = lagrange(points_in[1, rows, :])
        lz = lagrange(points_in[2, rows, :])
        sums = [None] * 3
        for i in range(3):
            inner = [None] * 3
            for j in range(3):
                for c in range(3):
                    n = c * 27 + 9 * i + 3 * j
                    line = (
                        coefficients[n : n + 1, :] * lz[0]
                        + coefficients[n + 1 : n + 2, :] * lz[1]
                        + coefficients[n + 2 : n + 3, :] * lz[2]
                    ) * ly[j]
                    inner[c] = line if inner[c] is None else inner[c] + line
            for c in range(3):
                term = inner[c] * lx[i]
                sums[c] = term if sums[c] is None else sums[c] + term
        for c in range(3):
            out[c, rows, :] = base[c, rows, :] + scale * sums[c]
        return carry

    lax.fori_loop(0, markers // group, step, 0)


def trip(
    n_lat, n_rad, capacity, padded,
    pos, fld, vel, tags,
    final,
    coef, midway, landed, phi, table, request, asked, answer, answered, outgoing, arrived, onward,
    send_sem, recv_sem,
):
    lat, rad = lax.axis_index("lat"), lax.axis_index("rad")
    slots = 3 * n_rad
    places = slots * capacity
    markers, fields, blocks = fld.shape
    owned = vel.shape[1]
    chunks = outgoing.shape[1]

    def partner(k, q, back):
        by = (1 - k) if back else (k - 1)
        return lax.rem(lat + by + n_lat, n_lat), q

    barrier = pltpu.get_barrier_semaphore()
    for k in range(3):

        def greet(dq, carry, k=k):
            q = lax.rem(rad + dq, n_rad)
            pl.semaphore_signal(
                barrier, inc=1, device_id=partner(k, q, False), device_id_type=MESH
            )
            return carry

        lax.fori_loop(1 if k == 1 else 0, n_rad, greet, 0)

    def exchange(phase, source, target, size, back=False):
        for k in (0, 2, 1):

            def send(dq, carry, k=k):
                q = lax.rem(rad + dq, n_rad)
                pltpu.make_async_remote_copy(
                    src_ref=source.at[pl.ds((k * n_rad + q) * size, size)],
                    dst_ref=target.at[pl.ds((k * n_rad + rad) * size, size)],
                    send_sem=send_sem.at[phase],
                    recv_sem=recv_sem.at[phase],
                    device_id=partner(k, q, back),
                    device_id_type=MESH,
                ).start()
                return carry

            lax.fori_loop(1 if k == 1 else 0, n_rad, send, 0)
        own = pl.ds((n_rad + rad) * size, size)
        pltpu.make_async_copy(source.at[own], target.at[own], recv_sem.at[phase]).start()

    def await_arrivals(phase, target):
        pltpu.make_async_copy(target, target, recv_sem.at[phase]).wait()

    def await_sends(phase, source, size):
        part = source.at[pl.ds(0, (slots - 1) * size)]
        pltpu.make_async_copy(part, part, send_sem.at[phase]).wait()

    rows = slots * padded
    padded_rows = lax.broadcasted_iota(jnp.int32, (rows, blocks), 0)
    spread = (padded_rows == tags[3:4, :]).astype(jnp.float32).astype(jnp.bfloat16)
    wanted = (tags[1:2, :] + 1).astype(jnp.float32)
    column = lax.broadcasted_iota(jnp.int32, (LANES, blocks), 0)
    labels = jnp.where(column == 0, wanted, 0.0)
    request[...] = dot(spread, labels.astype(jnp.bfloat16), ((1,), (1,))).reshape(
        slots, padded, LANES
    )
    pl.semaphore_wait(barrier, slots - 1)
    exchange(0, request, asked, 1)

    vel_high, vel_low = split(vel[...])
    element = lax.broadcasted_iota(jnp.int32, (owned, blocks), 0)
    pick = (element == tags[0:1, :]).astype(jnp.float32).astype(jnp.bfloat16)
    coef[...] = dot(vel_high, pick, ((1,), (0,))) + dot(vel_low, pick, ((1,), (0,)))
    advance(pos, coef, pos, midway, 0.5 * time_step, 16)

    await_arrivals(0, asked)
    wish = asked[...].reshape(rows, LANES)[:, 0:1].astype(jnp.int32)
    pick = (lax.broadcasted_iota(jnp.int32, (rows, owned), 1) + 1 == wish)
    pick = pick.astype(jnp.float32).astype(jnp.bfloat16)
    answer[...] = (
        dot(pick, vel_high, ((1,), (1,))) + dot(pick, vel_low, ((1,), (1,)))
    ).reshape(slots, padded, LANES)
    exchange(1, answer, answered, 1, back=True)
    await_arrivals(1, answered)
    high, low = split(answered[...].reshape(rows, LANES))
    coef[...] = dot(high, spread, ((0,), (0,))) + dot(low, spread, ((0,), (0,)))
    advance(midway, coef, pos, landed, time_step, 16)

    group = 8

    def tabulate(g, sums):
        part = pl.ds(pl.multiple_of(g * group, group), group)
        lx = lagrange(landed[0, part, :])
        ly = lagrange(landed[1, part, :])
        lz = lagrange(landed[2, part, :])
        new = []
        for i in range(3):
            for j in range(3):
                xy = lx[i] * ly[j]
                for k in range(3):
                    value = xy * lz[k]
                    n = 9 * i + 3 * j + k
                    phi[n, part, :] = value
                    new.append(sums[n] + value * value)
        return tuple(new)

    zero = jnp.zeros((group, blocks), jnp.float32)
    squares = lax.fori_loop(0, markers // group, tabulate, (zero,) * 27)
    first = 3 * markers
    table[pl.ds(0, first), :] = landed[...].reshape(first, blocks)
    base = first + 27 * fields
    table[pl.ds(base, table.shape[0] - base), :] = jnp.zeros(
        (table.shape[0] - base, blocks), jnp.float32
    )
    for n in range(27):
        table[base + n : base + n + 1, :] = jnp.sum(squares[n], axis=0, keepdims=True)
    table[base + 27 : base + 28, :] = (tags[2:3, :] + 1).astype(jnp.float32)
    table[base + 28 : base + 29, :] = (tags[5:6, :] + 1).astype(jnp.float32)
    for i in range(3):

        def gather(g, sums, i=i):
            for s in range(8):
                m = g * 8 + s
                carried = fld[m]
                sums = tuple(
                    sums[j] + phi[9 * i + j, pl.ds(m, 1), :] * carried for j in range(9)
                )
            return sums

        zero = jnp.zeros((fields, blocks), jnp.float32)
        sums = lax.fori_loop(0, markers // 8, gather, (zero,) * 9)
        for j in range(9):
            start = first + (9 * i + j) * fields
            table[start : start + fields, :] = sums[j]

    place = lax.broadcasted_iota(jnp.int32, (places, blocks), 0)
    spread = (place == tags[4:5, :]).astype(jnp.float32).astype(jnp.bfloat16)
    for j in range(chunks):
        high, low = split(table[pl.ds(j * LANES, LANES), :])
        outgoing[:, j, :] = dot(spread, high, ((1,), (1,))) + dot(spread, low, ((1,), (1,)))
    exchange(2, outgoing, arrived, capacity)
    await_arrivals(2, arrived)

    where_to, lane = divmod(base + 28, LANES)
    target = arrived[:, where_to, :][:, lane : lane + 1].astype(jnp.int32)
    turn = lax.broadcasted_iota(jnp.int32, (places, places), 1) + 1 == target
    turn = turn.astype(jnp.float32).T.astype(jnp.bfloat16)
    for j in range(chunks):
        high, low = split(arrived[:, j, :])
        onward[:, j, :] = dot(turn, high, ((1,), (0,))) + dot(turn, low, ((1,), (0,)))
    exchange(3, onward, final, capacity)
    await_arrivals(3, final)
    await_sends(0, request, 1)
    await_sends(1, answer, 1)
    await_sends(2, outgoing, capacity)
    await_sends(3, onward, capacity)


def settle(fields, markers, final, moved, projected):
    places = final.shape[0]
    owned = projected.shape[2]
    first = 3 * markers // LANES
    base = 27 * fields
    chunks = final.shape[1]
    moved[...] = final[:, 0:3, :]
    at, lane = divmod(3 * markers + base + 27, LANES)
    element = final[:, at, :][:, lane : lane + 1].astype(jnp.int32)
    hits = lax.broadcasted_iota(jnp.int32, (places, owned), 1) + 1 == element
    hits = hits.astype(jnp.float32).astype(jnp.bfloat16)
    sums = []
    for j in range(first, chunks):
        high, low = split(final[:, j, :].T)
        sums.append(dot(high, hits, ((1,), (0,))) + dot(low, hits, ((1,), (0,))))
    sums = jnp.concatenate(sums, axis=0)
    inverse = 1.0 / (1.0 + sums[base : base + 27, :])
    for n in range(27):
        projected[n] = sums[n * fields : (n + 1) * fields, :] * inverse[n : n + 1, :]


def per_device(n_lat, n_rad, positions, fields, velocity, counts, elements, routes):
    blocks, _, markers = positions.shape
    n_fields = fields.shape[1]
    capacity = max(1, 2 * blocks // (3 * n_rad))
    slots = 3 * n_rad
    places = slots * capacity
    padded = round_up(capacity, 8)
    owned = velocity.shape[1]
    chunks = round_up(3 * markers + 27 * n_fields + 29, LANES) // LANES
    live = jnp.arange(blocks, dtype=jnp.int32) < counts[0]
    wide = jnp.where(live, routes[0] // capacity * padded + routes[0] % capacity, -1)
    tags = jnp.concatenate(
        [elements, wide[None], jnp.where(live, routes[0], -1)[None], routes[1:2],
         jnp.zeros((2, blocks), jnp.int32)], axis=0
    )
    pos = jnp.transpose(positions, (1, 2, 0))
    fld = jnp.transpose(fields.astype(jnp.float32), (2, 1, 0))
    vel = jnp.pad(velocity, ((0, LANES - velocity.shape[0]), (0, 0)))
    f32 = jnp.float32
    vmem = pl.BlockSpec(memory_space=pltpu.VMEM)
    small = pltpu.VMEM((slots, padded, LANES), f32)
    large = pltpu.VMEM((places, chunks, LANES), f32)
    final = pl.pallas_call(
        functools.partial(trip, n_lat, n_rad, capacity, padded),
        out_shape=jax.ShapeDtypeStruct((places, chunks, LANES), f32),
        in_specs=[vmem] * 4,
        out_specs=vmem,
        scratch_shapes=[
            pltpu.VMEM((LANES, blocks), f32),
            pltpu.VMEM((3, markers, blocks), f32),
            pltpu.VMEM((3, markers, blocks), f32),
            pltpu.VMEM((27, markers, blocks), f32),
            pltpu.VMEM((chunks * LANES, blocks), f32),
            small, small, small, small,
            large, large, large,
            pltpu.SemaphoreType.DMA((4,)),
            pltpu.SemaphoreType.DMA((4,)),
        ],
        compiler_params=pltpu.CompilerParams(collective_id=0, has_side_effects=True),
        name="trip",
    )(pos, fld, vel, tags)
    return pl.pallas_call(
        functools.partial(settle, n_fields, markers),
        out_shape=(
            jax.ShapeDtypeStruct((places, 3, markers), f32),
            jax.ShapeDtypeStruct((27, n_fields, owned), f32),
        ),
        in_specs=[vmem],
        out_specs=(vmem, vmem),
        name="settle",
    )(final)


def solution(mesh):
    in_specs = (
        P(("lat", "rad"), None, None),
        P(("lat", "rad"), None, None),
        P(None, ("lat", "rad")),
        P(("lat", "rad")),
        P(None, ("lat", "rad")),
        P(None, ("lat", "rad")),
    )
    out_specs = (P(("lat", "rad"), None, None), P(None, None, ("lat", "rad")))
    return jax.shard_map(
        functools.partial(per_device, mesh.shape["lat"], mesh.shape["rad"]),
        mesh=mesh, in_specs=in_specs, out_specs=out_specs, check_vma=False,
    )
```

time: 183 us -> 71.4 us (0.39)
  waiting for transfers between devices: 62.9 us -> 0 us
  Pallas kernels: 0 us -> 60.8 us
  starting transfers between devices: 50.8 us -> 0 us
  local copies, waits for them, and re-layouts: 33.4 us -> 7.1 us
  matrix products: 16.5 us -> 0 us
  other arithmetic: 16.6 us -> 1.82 us
    pallas_call x0 -> x2, Pallas kernels: none -> 60.8 us  [the longest x1 57.8 us: per_device(): pl.pallas_call(functools.partial(trip, n_lat, n_rad, capacity, padded), o...]
    ppermute x14 -> x0, waiting for transfers between devices: 49.3 us -> none  [passed_along(): return lax.ppermute(x, axis, [(i, (i + by) % size) for i in range(size)])]
    all_to_all x7 -> x0, starting transfers between devices: 28.8 us -> none  [migrate(): lax.all_to_all(shaped, 'rad', split_axis=1, concat_axis=1, tiled=True)]
    ppermute x14 -> x0, starting transfers between devices: 22 us -> none  [passed_along(): return lax.ppermute(x, axis, [(i, (i + by) % size) for i in range(size)])]
    dot_general x5 -> x0, matrix products: 16.5 us -> none  [the longest x1 8.16 us: block_sums(): moments = jnp.einsum('snb,sfb->snf', shapes, carried, precision=exact)]
    all_to_all x7 -> x0, waiting for transfers between devices: 13.6 us -> none  [migrate(): lax.all_to_all(shaped, 'rad', split_axis=1, concat_axis=1, tiled=True)]
    gather x14 -> x0, local copies, waits for them, and re-layouts: 11.7 us -> none  [the longest x12 10.3 us: arrange(): picked = jnp.take(member, source, axis=0)]
    unnamed x18 -> x4, local copies, waits for them, and re-layouts: 8.14 us -> 2.48 us
  transfers between devices with their start and end apart: 21 -> 0, of which waited for: 10 -> 0; matrix products, arithmetic and copies ran while one was open for 31% -> 0% of each run, Pallas kernels for 0% -> 0%
where the time goes in v1:
time: 71.4 us; the launch traced here: 71 us
  Pallas kernels  60.8 us (85%)
  local copies, waits for them, and re-layouts  7.1 us (10%)
  other arithmetic  1.82 us (3%)
  between operations  1.37 us (2%)
    pallas_call x1, Pallas kernels, per_device(): pl.pallas_call(functools.partial(trip, n_lat, n_rad, capacity, padded), o...  57.8 us
    pallas_call x1, Pallas kernels, per_device(): pl.pallas_call(functools.partial(settle, n_fields, markers), out_shape=(j...  2.94 us
    unnamed x4, local copies, waits for them, and re-layouts  2.48 us
    pallas_call x1, local copies, waits for them, and re-layouts, per_device(): pl.pallas_call(functools.partial(settle, n_fields, markers), out_shape=(j...  1.79 us
    pad x1, local copies, waits for them, and re-layouts, per_device(): vel = jnp.pad(velocity, ((0, LANES - velocity.shape[0]), (0, 0)))  1.55 us

profile of v1, /device:TPU:0, one launch (start us, length us, event | category | flops | bytes accessed | tf_op | source)
XLA Modules:
  0.0 71.0 jit_solution(13522278749468906196)
XLA Ops:
  0.6 0.0 copy-start
  1.3 0.8 %fusion.1 = (s32[1,128]{1,0:T(1,128)S(1)}, s32[1,128]{1,0:T(1,128)S(1)}, s32[1,128]{1,0:T(1,128)S(1)}) fusion(s32[2,128]{1,0:T(2,128)} %param.11, s32[]{:T(128)} %bitcast.4), kind=kLoop, calls=%fused_computation.6 | loop fusion | flops 2176 | bytes 2564 | tf_op jit(solution)/shard_map/slice | solution.py:253
  2.1 1.3 %concatenate.3.tags = s32[8,128]{1,0:T(8,128)} concatenate(s32[3,128]{1,0:T(4,128)} %param.10, s32[1,128]{1,0:T(1,128)S(1)} %get-tuple-element.5, s32[1,128]{1,0:T(1,128)S(1)} %get-tuple-element.6, s32[1,128]{1,0:T(1,128)S(1)} %get-tuple-element.4, s32[2,128]{1,0:T(2,128)S(1)} %broadcast_in_dim.8), dimensions={0} | concatenate | bytes 8192 | tf_op jit(solution)/shard_map/concatenate | solution.py:252
  3.4 1.6 %pad.4.vel = f32[128,256]{1,0:T(8,128)} pad(f32[81,256]{1,0:T(8,128)} %param.8, f32[]{:T(128)} %constant.21.clone.1), padding=0_47x0_0 | pad | bytes 214020 | tf_op jit(solution)/shard_map/jit(_pad)/pad | solution.py:258
  5.0 1.7 %copy.8 = f32[128,3,128]{0,2,1:T(8,128)} copy(f32[128,3,128]{2,0,1:T(8,128)} %param.6) | data formatting | bytes 393216 | tf_op args[0]
  6.7 0.0 copy-done
  6.7 0.7 %copy.9 = bf16[128,16,128]{0,1,2:T(8,128)(2,1)S(1)} copy(bf16[128,16,128]{2,1,0:T(8,128)(2,1)S(1)} %copy-done) | data formatting | bytes 1048576 | tf_op args[1]
  7.4 1.0 %convert_bitcast_fusion.fld = f32[128,16,128]{2,1,0:T(8,128)} fusion(bf16[128,16,128]{0,1,2:T(8,128)(2,1)S(1)} %copy.9), kind=kLoop, calls=%fused_computation | loop fusion | flops 262144 | bytes 1572864 | tf_op jit(solution)/shard_map/transpose | solution.py:257
  8.5 57.8 %trip.1.final = f32[240,7,128]{2,1,0:T(8,128)} custom-call(f32[3,128,128]{2,1,0:T(8,128)} %bitcast.5, f32[128,16,128]{2,1,0:T(8,128)} %convert_bitcast_fusion.fld, f32[128,256]{1,0:T(8,128)} %pad.4.vel, s32[8,128]{1,0:T(8,128)} %concatenate.3.tags), custom_call_target="tpu_custom_call" | custom-call | tf_op jit(solution)/shard_map/trip/pallas_call | solution.py:263
  66.3 2.9 %settle.1 = (f32[240,3,128]{2,1,0:T(4,128)}, f32[27,16,256]{2,1,0:T(8,128)}) custom-call(f32[240,7,128]{2,1,0:T(8,128)} %trip.1.final), custom_call_target="tpu_custom_call" | custom-call | tf_op jit(solution)/shard_map/settle/pallas_call | solution.py:282
  69.3 1.8 %copy.10 = f32[240,3,128]{2,0,1:T(8,128)} copy(f32[240,3,128]{2,1,0:T(4,128)} %get-tuple-element.2) | data formatting | bytes 737280 | tf_op jit(solution)/shard_map/settle/pallas_call | solution.py:282
  (1 shorter events, 0.0 us)
Async XLA Ops:
  0.6 6.1 %copy-start = (bf16[128,16,128]{2,1,0:T(8,128)(2,1)S(1)}, bf16[128,16,128]{2,1,0:T(8,128)(2,1)}, u32[]{:S(2)}) copy-start(bf16[128,16,128]{2,1,0:T(8,128)(2,1)} %param.7) | copy-start | bytes 1572868

commit v2 on v1

v2 whole, which is shorter than its diff:
```python
import functools

import jax
import jax.numpy as jnp
from jax import lax
from jax.experimental import pallas as pl
from jax.experimental.pallas import tpu as pltpu
from jax.sharding import PartitionSpec as P

time_step = 0.4
MESH = pl.DeviceIdType.MESH
LANES = 128


def round_up(x, by):
    return -(-x // by) * by


def split(x):
    high = x.astype(jnp.bfloat16)
    low = (x - high.astype(jnp.float32)).astype(jnp.bfloat16)
    return high, low


def dot(a, b, dims):
    return lax.dot_general(a, b, (dims, ((), ())), preferred_element_type=jnp.float32)


def lagrange(s):
    return (2.0 * (s - 0.5) * (s - 1.0), -4.0 * s * (s - 1.0), 2.0 * s * (s - 0.5))


def advance(points_in, coefficients, base, out, scale, group):
    markers = base.shape[1]

    def step(g, carry):
        rows = pl.ds(pl.multiple_of(g * group, group), group)
        lx = lagrange(points_in[0, rows, :])
        ly = lagrange(points_in[1, rows, :])
        lz = lagrange(points_in[2, rows, :])
        sums = [None] * 3
        for i in range(3):
            inner = [None] * 3
            for j in range(3):
                for c in range(3):
                    n = c * 27 + 9 * i + 3 * j
                    line = (
                        coefficients[n : n + 1, :] * lz[0]
                        + coefficients[n + 1 : n + 2, :] * lz[1]
                        + coefficients[n + 2 : n + 3, :] * lz[2]
                    ) * ly[j]
                    inner[c] = line if inner[c] is None else inner[c] + line
            for c in range(3):
                term = inner[c] * lx[i]
                sums[c] = term if sums[c] is None else sums[c] + term
        for c in range(3):
            out[c, rows, :] = base[c, rows, :] + scale * sums[c]
        return carry

    lax.fori_loop(0, markers // group, step, 0)


def trip(
    n_lat, n_rad, capacity,
    counts, pos, vel, elements, routes, fld,
    *rest,
):
    final, rest = rest[:3], rest[3:]
    raw, wide, carried, start_points, coef, midway, landed, phi, table = rest[:9]
    request, asked, answer, answered = rest[9:13]
    outgoing, arrived, onward = rest[13:16], rest[16:19], rest[19:22]
    load_sem, send_sem, recv_sem = rest[22:]
    lat, rad = lax.axis_index("lat"), lax.axis_index("rad")
    slots = 3 * n_rad
    places = slots * capacity
    blocks, fields, markers = fld.shape
    owned = vel.shape[1]
    bf16, f32 = jnp.bfloat16, jnp.float32
    load = pltpu.make_async_copy(fld, raw, load_sem)
    load.start()

    def partner(k, q, back):
        by = (1 - k) if back else (k - 1)
        return lax.rem(lat + by + n_lat, n_lat), q

    barrier = pltpu.get_barrier_semaphore()
    for k in range(3):

        def greet(dq, carry, k=k):
            q = lax.rem(rad + dq, n_rad)
            pl.semaphore_signal(
                barrier, inc=1, device_id=partner(k, q, False), device_id_type=MESH
            )
            return carry

        lax.fori_loop(1 if k == 1 else 0, n_rad, greet, 0)

    def exchange(phase, source, target, size, back=False):
        for k in (0, 2, 1):

            def send(dq, carry, k=k):
                q = lax.rem(rad + dq, n_rad)
                pltpu.make_async_remote_copy(
                    src_ref=source.at[pl.ds((k * n_rad + q) * size, size)],
                    dst_ref=target.at[pl.ds((k * n_rad + rad) * size, size)],
                    send_sem=send_sem.at[phase],
                    recv_sem=recv_sem.at[phase],
                    device_id=partner(k, q, back),
                    device_id_type=MESH,
                ).start()
                return carry

            lax.fori_loop(1 if k == 1 else 0, n_rad, send, 0)
        own = pl.ds((n_rad + rad) * size, size)
        pltpu.make_async_copy(source.at[own], target.at[own], recv_sem.at[phase]).start()

    def await_arrivals(phase, target):
        pltpu.make_async_copy(target, target, recv_sem.at[phase]).wait()

    def await_sends(phase, source, size):
        part = source.at[pl.ds(0, (slots - 1) * size)]
        pltpu.make_async_copy(part, part, send_sem.at[phase]).wait()

    def iota(shape, axis):
        return lax.broadcasted_iota(jnp.int32, shape, axis)

    def slot_of(place):
        return jnp.floor((place.astype(f32) + 0.5) * (1.0 / capacity)).astype(jnp.int32)

    def mask(condition):
        return condition.astype(f32).astype(bf16)

    route = jnp.where(iota((1, blocks), 1) < counts[0], routes[0:1, :], -1)
    slot = slot_of(route)
    sent_to = iota((slots, blocks), 0) == slot
    within = mask(iota((LANES, blocks), 0) == route - slot * capacity)
    for row, label in enumerate((elements[1:2, :], routes[1:2, :])):
        marked = jnp.where(sent_to, (label + 1).astype(f32), 0.0).astype(bf16)
        request[:, row, :] = dot(marked, within, ((1,), (1,)))
    pl.semaphore_wait(barrier, slots - 1)
    exchange(0, request, asked, 1)

    for c in range(3):
        start_points[c] = pos[c].T
    vel_high, vel_low = split(vel[...])
    pick = mask(iota((owned, blocks), 0) == elements[0:1, :])
    coef[...] = dot(vel_high, pick, ((1,), (0,))) + dot(vel_low, pick, ((1,), (0,)))
    advance(start_points, coef, start_points, midway, 0.5 * time_step, 16)
    spread = mask(iota((places, blocks), 0) == route)

    own_slot = slot_of(iota((places, slots), 0))
    by_slot = mask(own_slot == iota((places, slots), 1))
    lane = iota((places, LANES), 0) - slot_of(iota((places, LANES), 0)) * capacity
    by_lane = lane == iota((places, LANES), 1)

    def label_column(row):
        lines = dot(by_slot, asked[:, row, :].astype(bf16), ((1,), (0,)))
        return jnp.sum(jnp.where(by_lane, lines, 0.0), axis=1, keepdims=True).astype(jnp.int32)

    await_arrivals(0, asked)
    pick = mask(iota((places, owned), 1) + 1 == label_column(0))
    answer[:, 0, 0 : vel.shape[0]] = dot(pick, vel_high, ((1,), (1,))) + dot(
        pick, vel_low, ((1,), (1,))
    )
    answer[:, 0, vel.shape[0] :] = jnp.zeros((places, LANES - vel.shape[0]), f32)
    exchange(1, answer, answered, capacity, back=True)
    turn = (iota((places, places), 1) + 1 == label_column(1)).astype(f32).T.astype(bf16)
    load.wait()
    wide[...] = raw[...].astype(f32)
    for f in range(fields):
        carried[:, f, :] = wide[:, f, :].T
    await_arrivals(1, answered)
    high, low = split(answered[:, 0, 0 : vel.shape[0]])
    coef[...] = dot(high, spread, ((0,), (0,))) + dot(low, spread, ((0,), (0,)))
    advance(midway, coef, start_points, landed, time_step, 16)

    group = 8

    def tabulate(g, sums):
        part = pl.ds(pl.multiple_of(g * group, group), group)
        lx = lagrange(landed[0, part, :])
        ly = lagrange(landed[1, part, :])
        lz = lagrange(landed[2, part, :])
        new = []
        for i in range(3):
            for j in range(3):
                xy = lx[i] * ly[j]
                for k in range(3):
                    value = xy * lz[k]
                    n = 9 * i + 3 * j + k
                    phi[n, part, :] = value
                    new.append(sums[n] + value * value)
        return tuple(new)

    zero = jnp.zeros((group, blocks), f32)
    squares = lax.fori_loop(0, markers // group, tabulate, (zero,) * 27)

    def moments(nodes, first):
        def gather(g, sums):
            for s in range(8):
                m = g * 8 + s
                values = carried[m]
                sums = tuple(
                    total + phi[n, pl.ds(m, 1), :] * values for total, n in zip(sums, nodes)
                )
            return sums

        zero = jnp.zeros((fields, blocks), f32)
        sums = lax.fori_loop(0, markers // 8, gather, (zero,) * len(nodes))
        for index, total in enumerate(sums):
            table[first + index * fields : first + (index + 1) * fields, :] = total

    def put(buffer, j, rows):
        high, low = split(rows)
        buffer[:, j, :] = dot(spread, high, ((1,), (1,))) + dot(spread, low, ((1,), (1,)))

    per_row = LANES // fields
    full = 27 // per_row
    last = tuple(range(full * per_row, 27))
    moments(last, 0)
    base = len(last) * fields
    table[base:LANES, :] = jnp.zeros((LANES - base, blocks), f32)
    for n in range(27):
        table[base + n : base + n + 1, :] = jnp.sum(squares[n], axis=0, keepdims=True)
    table[base + 27 : base + 28, :] = (elements[2:3, :] + 1).astype(f32)
    for c in range(3):
        put(outgoing[0], c, landed[c])
    put(outgoing[0], 3, table[0:LANES, :])
    exchange(2, outgoing[0], arrived[0], capacity)
    node = 0
    for part in (1, 2):
        for j in range(outgoing[part].shape[1]):
            moments(tuple(range(node, node + per_row)), 0)
            node += per_row
            put(outgoing[part], j, table[0:LANES, :])
        exchange(2 + part, outgoing[part], arrived[part], capacity)

    for part in range(3):
        await_arrivals(2 + part, arrived[part])
        for j in range(arrived[part].shape[1]):
            high, low = split(arrived[part][:, j, :])
            onward[part][:, j, :] = dot(turn, high, ((1,), (0,))) + dot(turn, low, ((1,), (0,)))
        exchange(5 + part, onward[part], final[part], capacity)
    for part in range(3):
        await_arrivals(5 + part, final[part])
    await_sends(0, request, 1)
    await_sends(1, answer, capacity)
    for part in range(3):
        await_sends(2 + part, outgoing[part], capacity)
        await_sends(5 + part, onward[part], capacity)


def settle(fields, first, second, third, moved, projected):
    places = first.shape[0]
    owned = projected.shape[2]
    per_row = LANES // fields
    base = (27 - 27 // per_row * per_row) * fields
    for c in range(3):
        moved[c] = first[:, c, :]
    element = first[:, 3, :][:, base + 27 : base + 28].astype(jnp.int32)
    hits = lax.broadcasted_iota(jnp.int32, (places, owned), 1) + 1 == element
    hits = hits.astype(jnp.float32).astype(jnp.bfloat16)

    def total(lines):
        high, low = split(lines.T)
        return dot(high, hits, ((1,), (0,))) + dot(low, hits, ((1,), (0,)))

    tail = total(first[:, 3, :])
    inverse = 1.0 / (1.0 + tail[base : base + 27, :])
    node = 0
    for part in (second, third):
        for j in range(part.shape[1]):
            sums = total(part[:, j, :])
            for n in range(per_row):
                projected[node] = sums[n * fields : (n + 1) * fields, :] * inverse[node : node + 1, :]
                node += 1
    for n in range(27 - node):
        projected[node + n] = (
            tail[n * fields : (n + 1) * fields, :] * inverse[node + n : node + n + 1, :]
        )


def per_device(n_lat, n_rad, positions, fields, velocity, counts, elements, routes):
    blocks, _, markers = positions.shape
    n_fields = fields.shape[1]
    capacity = max(1, 2 * blocks // (3 * n_rad))
    slots = 3 * n_rad
    places = slots * capacity
    owned = velocity.shape[1]
    full = 27 * n_fields // LANES
    f32 = jnp.float32
    vmem = pl.BlockSpec(memory_space=pltpu.VMEM)
    small = pltpu.VMEM((slots, 2, LANES), f32)
    line = pltpu.VMEM((places, 1, LANES), f32)
    points = pltpu.VMEM((3, markers, blocks), f32)
    shapes = [(places, 4, LANES), (places, full - 1, LANES), (places, 1, LANES)]
    parts = [pltpu.VMEM(shape, f32) for shape in shapes]
    final = pl.pallas_call(
        functools.partial(trip, n_lat, n_rad, capacity),
        out_shape=[jax.ShapeDtypeStruct(shape, f32) for shape in shapes],
        in_specs=[pl.BlockSpec(memory_space=pltpu.SMEM)] + [vmem] * 4
        + [pl.BlockSpec(memory_space=pl.ANY)],
        out_specs=[vmem] * 3,
        scratch_shapes=[
            pltpu.VMEM(fields.shape, fields.dtype),
            pltpu.VMEM(fields.shape, f32),
            pltpu.VMEM((markers, n_fields, blocks), f32),
            points,
            pltpu.VMEM((velocity.shape[0], blocks), f32),
            points,
            points,
            pltpu.VMEM((27, markers, blocks), f32),
            pltpu.VMEM((LANES, blocks), f32),
            small, small, line, line,
            *parts, *parts, *parts,
            pltpu.SemaphoreType.DMA,
            pltpu.SemaphoreType.DMA((8,)),
            pltpu.SemaphoreType.DMA((8,)),
        ],
        compiler_params=pltpu.CompilerParams(collective_id=0, has_side_effects=True),
        name="trip",
    )(counts, jnp.transpose(positions, (1, 0, 2)), velocity, elements, routes, fields)
    moved, projected = pl.pallas_call(
        functools.partial(settle, n_fields),
        out_shape=(
            jax.ShapeDtypeStruct((3, places, markers), f32),
            jax.ShapeDtypeStruct((27, n_fields, owned), f32),
        ),
        in_specs=[vmem] * 3,
        out_specs=(vmem, vmem),
        name="settle",
    )(*final)
    return jnp.transpose(moved, (1, 0, 2)), projected


def solution(mesh):
    in_specs = (
        P(("lat", "rad"), None, None),
        P(("lat", "rad"), None, None),
        P(None, ("lat", "rad")),
        P(("lat", "rad")),
        P(None, ("lat", "rad")),
        P(None, ("lat", "rad")),
    )
    out_specs = (P(("lat", "rad"), None, None), P(None, None, ("lat", "rad")))
    return jax.shard_map(
        functools.partial(per_device, mesh.shape["lat"], mesh.shape["rad"]),
        mesh=mesh, in_specs=in_specs, out_specs=out_specs, check_vma=False,
    )
```

time: 71.4 us -> 53 us (0.74)
  Pallas kernels: 60.8 us -> 51.6 us
  local copies, waits for them, and re-layouts: 7.1 us -> 0 us
  other arithmetic: 1.82 us -> 0 us
    pallas_call x2, Pallas kernels: 60.8 us -> 51.6 us  [the longest x1 48.6 us: per_device(): pl.pallas_call(functools.partial(trip, n_lat, n_rad, capacity), out_shape...]
    unnamed x4 -> x0, local copies, waits for them, and re-layouts: 2.48 us -> none
    pallas_call x1 -> x0, local copies, waits for them, and re-layouts: 1.79 us -> none  [per_device(): pl.pallas_call(functools.partial(settle, n_fields, markers), out_shape=(j...]
    pad x1 -> x0, local copies, waits for them, and re-layouts: 1.55 us -> none  [per_device(): vel = jnp.pad(velocity, ((0, LANES - velocity.shape[0]), (0, 0)))]
    concatenate x1 -> x0, local copies, waits for them, and re-layouts: 1.28 us -> none  [per_device(): jnp.concatenate([elements, wide[None], jnp.where(live, routes[0], -1)[Non...]
    transpose x1 -> x0, other arithmetic: 1.05 us -> none  [per_device(): fld = jnp.transpose(fields.astype(jnp.float32), (2, 1, 0))]
    slice x1 -> x0, other arithmetic: 0.77 us -> none  [per_device(): routes[1:2]]
where the time goes in v2:
time: 53 us; the launch traced here: 52.8 us
  Pallas kernels  51.6 us (97%)
  between operations  1.28 us (2%)
    pallas_call x1, Pallas kernels, per_device(): pl.pallas_call(functools.partial(trip, n_lat, n_rad, capacity), out_shape...  48.6 us
    pallas_call x1, Pallas kernels, per_device(): pl.pallas_call(functools.partial(settle, n_fields), out_shape=(jax.ShapeD...  2.97 us

profile of v2, /device:TPU:0, one launch (start us, length us, event | category | flops | bytes accessed | tf_op | source)
XLA Modules:
  0.0 52.8 jit_solution(18025471658528262212)
XLA Ops:
  1.3 48.6 %trip.1 = (f32[240,4,128]{2,1,0:T(4,128)}, f32[240,2,128]{2,1,0:T(2,128)}, f32[240,1,128]{2,1,0:T(1,128)}) custom-call(s32[1]{0:T(128)S(6)} %copy.8.counts, f32[3,128,128]{2,1,0:T(8,128)} %bitcast.2, f32[81,256]{1,0:T(8,128)} %vel.1, s32[3,128]{1,0:T(4,128)} %elements.1, s32[2,128]{1,0:T(2,128)} %routes.1, bf16[128,16,128]{2,1,0:T(8,128)(2,1)} %fld.1), custom_call_target="tpu_custom_call" | custom-call | tf_op jit(solution)/shard_map/trip/pallas_call | solution.py:298
  49.9 3.0 %settle.1 = (f32[3,240,128]{2,1,0:T(8,128)}, f32[27,16,256]{2,1,0:T(8,128)}) custom-call(f32[240,4,128]{2,1,0:T(4,128)} %get-tuple-element.7.first, f32[240,2,128]{2,1,0:T(2,128)} %get-tuple-element.8.second, f32[240,1,128]{2,1,0:T(1,128)} %get-tuple-element.9.third), custom_call_target="tpu_custom_call" | custom-call | tf_op jit(solution)/shard_map/settle/pallas_call | solution.py:323

commit v3 on v2

--- a/solution.py
+++ b/solution.py
@@ -148,6 +148,10 @@
     advance(start_points, coef, start_points, midway, 0.5 * time_step, 16)
     spread = mask(iota((places, blocks), 0) == route)
 
+    def put(buffer, j, rows):
+        high, low = split(rows)
+        buffer[:, j, :] = dot(spread, high, ((1,), (1,))) + dot(spread, low, ((1,), (1,)))
+
     own_slot = slot_of(iota((places, slots), 0))
     by_slot = mask(own_slot == iota((places, slots), 1))
     lane = iota((places, LANES), 0) - slot_of(iota((places, LANES), 0)) * capacity
@@ -174,6 +178,12 @@
     coef[...] = dot(high, spread, ((0,), (0,))) + dot(low, spread, ((0,), (0,)))
     advance(midway, coef, start_points, landed, time_step, 16)
 
+    for c in range(2):
+        put(outgoing[0], c, landed[c])
+    exchange(2, outgoing[0], arrived[0], capacity)
+    put(outgoing[1], 0, landed[2])
+    exchange(3, outgoing[1], arrived[1], capacity)
+
     group = 8
 
     def tabulate(g, sums):
@@ -210,10 +220,6 @@
         for index, total in enumerate(sums):
             table[first + index * fields : first + (index + 1) * fields, :] = total
 
-    def put(buffer, j, rows):
-        high, low = split(rows)
-        buffer[:, j, :] = dot(spread, high, ((1,), (1,))) + dot(spread, low, ((1,), (1,)))
-
     per_row = LANES // fields
     full = 27 // per_row
     last = tuple(range(full * per_row, 27))
@@ -223,17 +229,11 @@
     for n in range(27):
         table[base + n : base + n + 1, :] = jnp.sum(squares[n], axis=0, keepdims=True)
     table[base + 27 : base + 28, :] = (elements[2:3, :] + 1).astype(f32)
-    for c in range(3):
-        put(outgoing[0], c, landed[c])
-    put(outgoing[0], 3, table[0:LANES, :])
-    exchange(2, outgoing[0], arrived[0], capacity)
-    node = 0
-    for part in (1, 2):
-        for j in range(outgoing[part].shape[1]):
-            moments(tuple(range(node, node + per_row)), 0)
-            node += per_row
-            put(outgoing[part], j, table[0:LANES, :])
-        exchange(2 + part, outgoing[part], arrived[part], capacity)
+    put(outgoing[2], full, table[0:LANES, :])
+    for j in range(full):
+        moments(tuple(range(j * per_row, (j + 1) * per_row)), 0)
+        put(outgoing[2], j, table[0:LANES, :])
+    exchange(4, outgoing[2], arrived[2], capacity)
 
     for part in range(3):
         await_arrivals(2 + part, arrived[part])
@@ -255,9 +255,11 @@
     owned = projected.shape[2]
     per_row = LANES // fields
     base = (27 - 27 // per_row * per_row) * fields
-    for c in range(3):
-        moved[c] = first[:, c, :]
-    element = first[:, 3, :][:, base + 27 : base + 28].astype(jnp.int32)
+    moved[0] = first[:, 0, :]
+    moved[1] = first[:, 1, :]
+    moved[2] = second[:, 0, :]
+    full = third.shape[1] - 1
+    element = third[:, full, :][:, base + 27 : base + 28].astype(jnp.int32)
     hits = lax.broadcasted_iota(jnp.int32, (places, owned), 1) + 1 == element
     hits = hits.astype(jnp.float32).astype(jnp.bfloat16)
 
@@ -265,15 +267,14 @@
         high, low = split(lines.T)
         return dot(high, hits, ((1,), (0,))) + dot(low, hits, ((1,), (0,)))
 
-    tail = total(first[:, 3, :])
+    tail = total(third[:, full, :])
     inverse = 1.0 / (1.0 + tail[base : base + 27, :])
     node = 0
-    for part in (second, third):
-        for j in range(part.shape[1]):
-            sums = total(part[:, j, :])
-            for n in range(per_row):
-                projected[node] = sums[n * fields : (n + 1) * fields, :] * inverse[node : node + 1, :]
-                node += 1
+    for j in range(full):
+        sums = total(third[:, j, :])
+        for n in range(per_row):
+            projected[node] = sums[n * fields : (n + 1) * fields, :] * inverse[node : node + 1, :]
+            node += 1
     for n in range(27 - node):
         projected[node + n] = (
             tail[n * fields : (n + 1) * fields, :] * inverse[node + n : node + n + 1, :]
@@ -293,7 +294,7 @@
     small = pltpu.VMEM((slots, 2, LANES), f32)
     line = pltpu.VMEM((places, 1, LANES), f32)
     points = pltpu.VMEM((3, markers, blocks), f32)
-    shapes = [(places, 4, LANES), (places, full - 1, LANES), (places, 1, LANES)]
+    shapes = [(places, 2, LANES), (places, 1, LANES), (places, full + 1, LANES)]
     parts = [pltpu.VMEM(shape, f32) for shape in shapes]
     final = pl.pallas_call(
         functools.partial(trip, n_lat, n_rad, capacity),

time: 53 us -> 51.3 us (0.968)
  Pallas kernels: 51.6 us -> 49.8 us
    pallas_call x1, Pallas kernels: 48.6 us -> 46.9 us  [per_device(): pl.pallas_call(functools.partial(trip, n_lat, n_rad, capacity), out_shape...]
where the time goes in v3:
time: 51.3 us; the launch traced here: 51.1 us
  Pallas kernels  49.8 us (97%)
  between operations  1.28 us (2%)
    pallas_call x1, Pallas kernels, per_device(): pl.pallas_call(functools.partial(trip, n_lat, n_rad, capacity), out_shape...  46.9 us
    pallas_call x1, Pallas kernels, per_device(): pl.pallas_call(functools.partial(settle, n_fields), out_shape=(jax.ShapeD...  2.97 us

profile of v3, /device:TPU:0, one launch (start us, length us, event | category | flops | bytes accessed | tf_op | source)
XLA Modules:
  0.0 51.1 jit_solution(14293426620643817998)
XLA Ops:
  1.3 46.9 %trip.1 = (f32[240,2,128]{2,1,0:T(2,128)}, f32[240,1,128]{2,1,0:T(1,128)}, f32[240,4,128]{2,1,0:T(4,128)}) custom-call(s32[1]{0:T(128)S(6)} %copy.8.counts, f32[3,128,128]{2,1,0:T(8,128)} %bitcast.2, f32[81,256]{1,0:T(8,128)} %vel.1, s32[3,128]{1,0:T(4,128)} %elements.1, s32[2,128]{1,0:T(2,128)} %routes.1, bf16[128,16,128]{2,1,0:T(8,128)(2,1)} %fld.1), custom_call_target="tpu_custom_call" | custom-call | tf_op jit(solution)/shard_map/trip/pallas_call | solution.py:299
  48.2 3.0 %settle.1 = (f32[3,240,128]{2,1,0:T(8,128)}, f32[27,16,256]{2,1,0:T(8,128)}) custom-call(f32[240,2,128]{2,1,0:T(2,128)} %get-tuple-element.7.first, f32[240,1,128]{2,1,0:T(1,128)} %get-tuple-element.8.second, f32[240,4,128]{2,1,0:T(4,128)} %get-tuple-element.9.third), custom_call_target="tpu_custom_call" | custom-call | tf_op jit(solution)/shard_map/settle/pallas_call | solution.py:324
